TPU v7x, 32 devices: a whole 2x2x4 slice. The times are simulated.
32 devices in a mesh: grp: 2 (over x), dom: 16 (over z, y, core).
Axes of the slice: x: 2, y: 2, z: 4, core: 2. Of those that a mesh axis runs over, the one named last changes fastest.
Arguments:
- surplus: float32 [48, 64, 4096], P('grp', None, 'dom'), may hold values from -40 to 40
- levels: int32 [48, 3], P('grp'), may hold values from 0 to 3
Outputs:
- updated: float32 [48, 64, 4096], P('grp', None, 'dom')
- coefficients: float32 [48], replicated
All inputs are finite; a program needn't handle non-finite values.
Results may differ from a plain program's by a relative error of at most 0.0003.
Values sent between devices are 32-bit elements; how exact they have to be, the bound alone decides.
A program may use at most 64 MiB of HBM per device.

v0:
```python
import functools

import jax
import jax.numpy as jnp
from jax import lax
from jax.experimental import pallas as pl
from jax.experimental.pallas import tpu as pltpu
from jax.sharding import PartitionSpec as P

MESH = pl.DeviceIdType.MESH
ROWS = 8
BLOCK = 16
PIECES = 2
SPREAD = 4
F32 = jnp.float32


def radices_of(size):
    out = []
    while size > 1:
        for r in (4, 2, 3, 5, 7, size):
            if size % r == 0:
                out.append(r)
                size //= r
                break
    return out


def digits_of(sub):
    return (sub // 16).astype(F32), lax.rem(sub // 4, 4).astype(F32), lax.rem(sub, 4).astype(F32)


def split3(x):
    hi = x.astype(jnp.bfloat16)
    rest = x - hi.astype(F32)
    mid = rest.astype(jnp.bfloat16)
    lo = (rest - mid.astype(F32)).astype(jnp.bfloat16)
    return jnp.concatenate([hi, mid, lo], axis=0)


def kernel(groups, radices, local, subs, surplus, levels, comb_out, coef_out, lev_out, *scratch):
    stages = len(radices)
    (xb, lev, lbc, prod, cbuf, local_sem, lev_send, lev_recv, x_send, x_recv, c_send, c_recv) = scratch[:12]
    slots = scratch[12:12 + stages]
    s_send = scratch[12 + stages:12 + 2 * stages]
    s_recv = scratch[12 + 2 * stages:12 + 3 * stages]
    grids = groups * local
    half = xb.shape[-1]
    chunks = subs // ROWS
    g = lax.axis_index("grp")
    d = lax.axis_index("dom")

    members = []
    stride = 1
    for t, r in enumerate(radices):
        digit = lax.rem(d // stride, r)
        base = d - digit * stride
        if t == 0:
            n = groups * r
            mine = g * r + digit
            device = functools.partial(lambda b, r_, q: (q // r_, b + lax.rem(q, r_)), base, r)
        else:
            n = r
            mine = digit
            device = functools.partial(lambda b, st, q: (g, b + q * st), base, stride)
        members.append((n, mine, device))
        stride *= r

    barrier = pltpu.get_barrier_semaphore()
    count = 0
    for n, mine, device in members:
        for k in range(1, n):
            q = lax.rem(mine + k, n)
            pl.semaphore_signal(barrier, inc=1, device_id=device(q), device_id_type=MESH)
            count += 1

    own_cells = pl.ds(pl.multiple_of(g * half, half), half)
    own_copy = pltpu.make_async_copy(
        surplus.at[:, :, own_cells], xb.at[pl.ds(g * local, local)], local_sem
    )
    own_copy.start()
    pl.semaphore_wait(barrier, count)

    def lev_copy(k):
        q = lax.rem(g + k, groups)
        return pltpu.make_async_remote_copy(
            src_ref=levels, dst_ref=lev.at[g], send_sem=lev_send.at[k], recv_sem=lev_recv.at[g],
            device_id=(q, d), device_id_type=MESH,
        )

    def x_copy(k, ch):
        q = lax.rem(g + k, groups)
        rows = pl.ds(pl.multiple_of(ch * ROWS, ROWS), ROWS)
        return pltpu.make_async_remote_copy(
            src_ref=surplus.at[:, rows, pl.ds(pl.multiple_of(q * half, half), half)],
            dst_ref=xb.at[pl.ds(g * local, local), rows],
            send_sem=x_send.at[k, ch], recv_sem=x_recv.at[g, ch],
            device_id=(q, d), device_id_type=MESH,
        )

    def x_arrival(k, ch):
        q = lax.rem(g + k, groups)
        rows = pl.ds(pl.multiple_of(ch * ROWS, ROWS), ROWS)
        block = xb.at[pl.ds(q * local, local), rows]
        return pltpu.make_async_remote_copy(
            src_ref=block, dst_ref=block, send_sem=x_send.at[k, ch], recv_sem=x_recv.at[q, ch],
            device_id=(q, d), device_id_type=MESH,
        )

    for k in range(1, groups):
        lev_copy(k).start()
    for ch in range(chunks):
        for k in range(1, groups):
            x_copy(k, ch).start()

    lev[g] = levels[...]
    for k in range(1, groups):
        q = lax.rem(g + k, groups)
        pltpu.make_async_remote_copy(
            src_ref=lev.at[q], dst_ref=lev.at[q], send_sem=lev_send.at[k], recv_sem=lev_recv.at[q],
            device_id=(q, d), device_id_type=MESH,
        ).wait_recv()
    lev_eye = lax.broadcasted_iota(jnp.int32, (local, local), 0) == lax.broadcasted_iota(
        jnp.int32, (local, local), 1
    )
    for h in range(groups):
        for axis in range(3):
            lev_row = lev[h, axis:axis + 1, :].astype(F32)
            lev_col = jnp.sum(jnp.where(lev_eye, lev_row, 0.0), axis=1, keepdims=True)
            lbc[axis, pl.ds(h * local, local), :] = jnp.broadcast_to(lev_col, (local, 128))
    lev_out[...] = lbc[:, pl.ds(pl.multiple_of(g * local, 8), local), :]
    prod[...] = jnp.zeros_like(prod)
    own_copy.wait()
    flat = xb.reshape(grids * subs, half)

    def gram_chunk(ch, carry):
        for k in range(1, groups):
            x_arrival(k, ch).wait_recv()
        lev0, lev1, lev2 = lbc[0], lbc[1], lbc[2]
        total = jnp.zeros(prod.shape, F32)
        for pair in range(0, ROWS, 2):
            parts = []
            for k in range(pair, pair + 2):
                s = ch * ROWS + k
                x = flat[pl.ds(s, grids, stride=subs), :]
                keep = (
                    (lev0 >= (s // 16).astype(F32))
                    & (lev1 >= lax.rem(s // 4, 4).astype(F32))
                    & (lev2 >= float(k % 4))
                )
                keep = jnp.concatenate([keep] * (half // 128), axis=1) if half > 128 else keep
                parts.append(jnp.where(keep, x, 0.0))
            y = split3(jnp.concatenate(parts, axis=1))
            total += lax.dot_general(y, y, (((1,), (1,)), ((), ())), preferred_element_type=F32)
        prod[...] += total
        return carry

    lax.fori_loop(0, chunks, gram_chunk, 0)

    part = prod[2 * grids:, :] + prod[grids:2 * grids, :] + prod[:grids, :]
    part = part[:, 2 * grids:] + part[:, grids:2 * grids] + part[:, :grids]
    value = jnp.concatenate([part, jnp.zeros((grids, 128 - grids), F32)], axis=1)
    fold = grids // 2
    value = value[:fold] + pltpu.roll(value[fold:], 64, 1)

    copies = []
    for t, (n, mine, device) in enumerate(members):
        buf, send, recv = slots[t], s_send[t], s_recv[t]
        buf[mine] = value
        for k in range(1, n):
            q = lax.rem(mine + k, n)
            copy = pltpu.make_async_remote_copy(
                src_ref=buf.at[mine], dst_ref=buf.at[mine], send_sem=send.at[k], recv_sem=recv.at[mine],
                device_id=device(q), device_id_type=MESH,
            )
            copy.start()
            copies.append(copy)
        for k in range(1, n):
            q = lax.rem(mine + k, n)
            pltpu.make_async_remote_copy(
                src_ref=buf.at[q], dst_ref=buf.at[q], send_sem=send.at[k], recv_sem=recv.at[q],
                device_id=device(q), device_id_type=MESH,
            ).wait_recv()
        value = buf[0]
        for q in range(1, n):
            value = value + buf[q]

    left = lax.broadcasted_iota(jnp.int32, (fold, 128), 1) < 64
    value = jnp.concatenate(
        [jnp.where(left, value, 0.0), jnp.where(left, pltpu.roll(value, 64, 1), 0.0)], axis=0
    )

    row = lax.broadcasted_iota(jnp.int32, (grids, 128), 0)
    col = lax.broadcasted_iota(jnp.int32, (grids, 128), 1)
    eye = row == col
    diag = jnp.where(eye, value, 0.0)
    diag_col = jnp.sum(diag, axis=1, keepdims=True) + 1e-06
    diag_row = jnp.sum(diag, axis=0, keepdims=True) + 1e-06
    scale_col = 1.0 / jnp.sqrt(diag_col)
    scale_row = 1.0 / jnp.sqrt(diag_row)
    system = scale_col * value * scale_row + jnp.where(eye, 0.1, 0.0)
    system = jnp.where(col == grids, jnp.sqrt(diag_col), jnp.where(col < grids, system, 0.0))
    for first in range(0, grids, BLOCK):
        width = min(BLOCK, grids - first)
        rows = [system[first + j:first + j + 1, :] for j in range(width)]
        cols = [
            jnp.broadcast_to(system[:, first + j:first + j + 1], (grids, 128)) for j in range(width)
        ]
        for j in range(width):
            k = first + j
            inverse = 1.0 / cols[j][k:k + 1, :]
            factor = jnp.where(row == k, 0.0, cols[j] * inverse)
            for m in range(j + 1, width):
                cols[m] = cols[m] - factor * cols[m][k:k + 1, :]
                rows[m] = rows[m] - factor[first + m:first + m + 1, :] * rows[j]
            system = system - factor * rows[j]
    final = jnp.sum(jnp.where(eye, system, 0.0), axis=1, keepdims=True)
    coef = scale_col * (system[:, grids:grids + 1] / final)
    coef_wide = jnp.broadcast_to(coef, (grids, 128))
    coef_out[...] = jnp.sum(jnp.where(eye, coef_wide, 0.0), axis=0, keepdims=True)[:, :grids]

    piece = subs // PIECES

    def c_copy(slot, k, p):
        block = cbuf.at[slot, pl.ds(p * piece, piece)]
        return pltpu.make_async_remote_copy(
            src_ref=block, dst_ref=block, send_sem=c_send.at[k, p], recv_sem=c_recv.at[slot, p],
            device_id=(lax.rem(g + k, groups), d), device_id_type=MESH,
        )

    for p in range(PIECES):
        sub = lax.broadcasted_iota(jnp.int32, (piece, half), 0) + p * piece
        dig0, dig1, dig2 = digits_of(sub)
        acc = jnp.zeros((piece, half), F32)
        for i in range(grids):
            keep = (
                (lbc[0, i:i + 1, 0:1] >= dig0)
                & (lbc[1, i:i + 1, 0:1] >= dig1)
                & (lbc[2, i:i + 1, 0:1] >= dig2)
            )
            acc += jnp.where(keep, coef_wide[i:i + 1, 0:1], 0.0) * xb[i, p * piece:(p + 1) * piece]
        cbuf[g, p * piece:(p + 1) * piece] = acc
        for k in range(1, groups):
            c_copy(g, k, p).start()
    for p in range(PIECES):
        for k in range(1, groups):
            c_copy(lax.rem(g + k, groups), k, p).wait_recv()
    for h in range(groups):
        comb_out[:, h * half:(h + 1) * half] = cbuf[h]

    for copy in copies:
        copy.wait_send()
    for k in range(1, groups):
        lev_copy(k).wait_send()
        for ch in range(chunks):
            x_copy(k, ch).wait_send()
        for p in range(PIECES):
            c_copy(g, k, p).wait_send()


def spread(combined, coef, lev, updated, coef_out, block, sems):
    local, subs, cells = updated.shape
    coef_out[...] = coef[...]
    dig0, dig1, dig2 = digits_of(lax.broadcasted_iota(jnp.int32, (subs, 128), 0))
    copies = []
    for i in range(local):
        keep = (lev[0, i:i + 1, :] >= dig0) & (lev[1, i:i + 1, :] >= dig1) & (lev[2, i:i + 1, :] >= dig2)
        for c in range(0, cells, 128):
            block[i, :, c:c + 128] = jnp.where(keep, combined[:, c:c + 128], 0.0)
        if (i + 1) % SPREAD == 0 or i + 1 == local:
            n = len(copies)
            part = pl.ds(n * SPREAD, i + 1 - n * SPREAD)
            copy = pltpu.make_async_copy(block.at[part], updated.at[part], sems.at[n])
            copy.start()
            copies.append(copy)
    for copy in copies:
        copy.wait()


def shards(groups, domains, surplus, levels):
    local, subs, cells = surplus.shape
    grids = groups * local
    half = cells // groups
    radices = radices_of(domains)
    sizes = [groups * r if t == 0 else r for t, r in enumerate(radices)]
    dma = pltpu.SemaphoreType.DMA
    chunks = subs // ROWS
    combined, coefficients, lev_wide = pl.pallas_call(
        functools.partial(kernel, groups, radices, local, subs),
        out_shape=(
            jax.ShapeDtypeStruct((subs, cells), F32),
            jax.ShapeDtypeStruct((1, grids), F32),
            jax.ShapeDtypeStruct((3, local, 128), F32),
        ),
        in_specs=[pl.BlockSpec(memory_space=pl.ANY), pl.BlockSpec(memory_space=pltpu.VMEM)],
        out_specs=tuple(pl.BlockSpec(memory_space=pltpu.VMEM) for _ in range(3)),
        scratch_shapes=[
            pltpu.VMEM((grids, subs, half), F32),
            pltpu.VMEM((groups, 3, local), jnp.int32),
            pltpu.VMEM((3, grids, 128), F32),
            pltpu.VMEM((3 * grids, 3 * grids), F32),
            pltpu.VMEM((groups, subs, half), F32),
            dma(()), dma((groups,)), dma((groups,)),
            dma((groups, chunks)), dma((groups, chunks)), dma((groups, PIECES)), dma((groups, PIECES)),
        ]
        + [pltpu.VMEM((n, grids // 2, 128), F32) for n in sizes]
        + [dma((n,)) for n in sizes]
        + [dma((n,)) for n in sizes],
        compiler_params=pltpu.CompilerParams(collective_id=0, has_side_effects=True),
    )(surplus, levels.T)
    updated, coefficients = pl.pallas_call(
        spread,
        out_shape=(
            jax.ShapeDtypeStruct((local, subs, cells), F32),
            jax.ShapeDtypeStruct((1, grids), F32),
        ),
        in_specs=[pl.BlockSpec(memory_space=pltpu.VMEM)] * 3,
        out_specs=(pl.BlockSpec(memory_space=pl.ANY), pl.BlockSpec(memory_space=pltpu.VMEM)),
        scratch_shapes=[pltpu.VMEM((local, subs, cells), F32), dma((-(-local // SPREAD),))],
    )(combined, coefficients, lev_wide)
    return (updated, coefficients.reshape(grids))


def solution(mesh):
    placed = (P("grp", None, "dom"), P("grp", None))
    return jax.shard_map(
        functools.partial(shards, mesh.shape["grp"], mesh.shape["dom"]),
        mesh=mesh, in_specs=placed, out_specs=(P("grp", None, "dom"), P()), check_vma=False,
    )
```

profile of v0, /device:TPU:0, one launch (start us, length us, event | category | flops | bytes accessed | tf_op | source)
XLA Modules:
  0.0 41.4 jit_solution(13250639285950382694)
XLA Ops:
  0.6 38.2 %shard_map.41 = (f32[64,256]{1,0:T(8,128)}, f32[1,48]{1,0:T(1,128)}, f32[3,24,128]{2,1,0:T(8,128)}) custom-call(f32[24,64,256]{2,1,0:T(8,128)} %surplus.1, s32[3,24]{1,0:T(4,128)} %bitcast.2), custom_call_target="tpu_custom_call" | custom-call | tf_op jit(solution)/shard_map/pallas_call | solution.py:288
  38.8 2.6 %shard_map.42 = (f32[24,64,256]{2,1,0:T(8,128)}, f32[1,48]{1,0:T(1,128)}) custom-call(f32[64,256]{1,0:T(8,128)} %get-tuple-element.7.combined, f32[1,48]{1,0:T(1,128)} %get-tuple-element.8.coef, f32[3,24,128]{2,1,0:T(8,128)} %get-tuple-element.9.lev), custom_call_target="tpu_custom_call" | custom-call | tf_op jit(solution)/shard_map/pallas_call | solution.py:311
where the time goes:
time: 41.6 us; the launch traced here: 41.4 us
  Pallas kernels  40.8 us (98%)
  between operations  0.64 us (2%)
    pallas_call x1, Pallas kernels, shards(): pl.pallas_call(functools.partial(kernel, groups, radices, local, subs), o...  38.2 us
    pallas_call x1, Pallas kernels, shards(): pl.pallas_call(spread, out_shape=(jax.ShapeDtypeStruct((local, subs, cell...  2.59 us

commit v1 on v0

--- a/solution.py
+++ b/solution.py
@@ -12,6 +12,9 @@
 BLOCK = 16
 PIECES = 2
 SPREAD = 4
+SLOT = 32
+STEP = 128
+VMEM_BYTES = 24 * 1024 * 1024
 F32 = jnp.float32
 
 
@@ -258,6 +261,357 @@
             c_copy(g, k, p).wait_send()
 
 
+def layout_of(groups, radices, g, d):
+    members = []
+    stride = 1
+    for t, r in enumerate(radices):
+        digit = lax.rem(d // stride, r)
+        base = d - digit * stride
+        if t == 0:
+            n = groups * r
+            mine = g * r + digit
+            device = functools.partial(lambda b, r_, q: (q // r_, b + lax.rem(q, r_)), base, r)
+        else:
+            n = r
+            mine = digit
+            device = functools.partial(lambda b, st, q: (g, b + q * st), base, stride)
+        members.append((n, mine, device))
+        stride *= r
+    return members
+
+
+def spread_out(members, t, buf, send, recv, value):
+    n, mine, device = members[t]
+    buf[mine] = value
+    copies = []
+    for k in range(1, n):
+        copy = pltpu.make_async_remote_copy(
+            src_ref=buf.at[mine], dst_ref=buf.at[mine], send_sem=send.at[k], recv_sem=recv.at[mine],
+            device_id=device(lax.rem(mine + k, n)), device_id_type=MESH,
+        )
+        copy.start()
+        copies.append(copy)
+    return copies
+
+
+def gather_in(members, t, buf, send, recv):
+    n, mine, device = members[t]
+    for k in range(1, n):
+        q = lax.rem(mine + k, n)
+        pltpu.make_async_remote_copy(
+            src_ref=buf.at[q], dst_ref=buf.at[q], send_sem=send.at[k], recv_sem=recv.at[q],
+            device_id=device(q), device_id_type=MESH,
+        ).wait_recv()
+
+
+def total_of(buf, first, last):
+    value = buf[first]
+    for q in range(first + 1, last):
+        value = value + buf[q]
+    return value
+
+
+def pack(square):
+    local = square.shape[0]
+    wide = jnp.concatenate([square, jnp.zeros((local, 128 - local), F32)], axis=1)
+    out = wide[:8]
+    for b in range(1, local // 8):
+        out = out + pltpu.roll(wide[8 * b:8 * b + 8], SLOT * b, 1)
+    return out
+
+
+def unpack(packed, local):
+    rows = [packed] + [pltpu.roll(packed, 128 - SLOT * b, 1) for b in range(1, local // 8)]
+    wide = jnp.concatenate(rows, axis=0)
+    return jnp.where(lax.broadcasted_iota(jnp.int32, (local, 128), 1) < local, wide, 0.0)
+
+
+def folded(products, n):
+    part = products[2 * n:, :] + products[n:2 * n, :] + products[:n, :]
+    return part[:, 2 * n:] + part[:, n:2 * n] + part[:, :n]
+
+
+def outer(a, b):
+    return lax.dot_general(a, b, (((1,), (1,)), ((), ())), preferred_element_type=F32)
+
+
+def count_dot(a, b):
+    bf16 = jnp.bfloat16
+    return jnp.dot(a.astype(bf16), b.astype(bf16), preferred_element_type=F32)
+
+
+def below(n, m, flip):
+    r = lax.broadcasted_iota(jnp.int32, (n, m), 0)
+    c = lax.broadcasted_iota(jnp.int32, (n, m), 1)
+    return jnp.where((r < c) if flip else (r > c), 1.0, 0.0)
+
+
+def solve(value, grids):
+    row = lax.broadcasted_iota(jnp.int32, (grids, 128), 0)
+    col = lax.broadcasted_iota(jnp.int32, (grids, 128), 1)
+    eye = row == col
+    diag = jnp.where(eye, value, 0.0)
+    diag_col = jnp.sum(diag, axis=1, keepdims=True) + 1e-06
+    diag_row = jnp.sum(diag, axis=0, keepdims=True) + 1e-06
+    scale_col = 1.0 / jnp.sqrt(diag_col)
+    scale_row = 1.0 / jnp.sqrt(diag_row)
+    system = scale_col * value * scale_row + jnp.where(eye, 0.1, 0.0)
+    system = jnp.where(col == grids, jnp.sqrt(diag_col), jnp.where(col < grids, system, 0.0))
+    for first in range(0, grids, BLOCK):
+        width = min(BLOCK, grids - first)
+        rows = [system[first + j:first + j + 1, :] for j in range(width)]
+        cols = [
+            jnp.broadcast_to(system[:, first + j:first + j + 1], (grids, 128)) for j in range(width)
+        ]
+        for j in range(width):
+            k = first + j
+            inverse = 1.0 / cols[j][k:k + 1, :]
+            factor = jnp.where(row == k, 0.0, cols[j] * inverse)
+            for m in range(j + 1, width):
+                cols[m] = cols[m] - factor * cols[m][k:k + 1, :]
+                rows[m] = rows[m] - factor[first + m:first + m + 1, :] * rows[j]
+            system = system - factor * rows[j]
+    final = jnp.sum(jnp.where(eye, system, 0.0), axis=1, keepdims=True)
+    coef = scale_col * (system[:, grids:grids + 1] / final)
+    return jnp.broadcast_to(coef, (grids, 128)), eye
+
+
+def sparse_kernel(groups, radices, local, subs, cap, surplus, levels, comb_out, coef_out, lev_out, fits_out, *scratch):
+    stages = len(radices)
+    (xb, xp, xs, csend, crecv, posb, lev, lbc, prod, cross, cbuf, local_sem, lev_sem, x_send, x_recv, c_send,
+     c_recv) = scratch[:17]
+    rest = [scratch[17 + m * stages:17 + (m + 1) * stages] for m in range(6)]
+    slots, s_send, s_recv, own_slots, o_send, o_recv = rest
+    grids = groups * local
+    half = xb.shape[-1]
+    chunks = cap // STEP
+    g = lax.axis_index("grp")
+    d = lax.axis_index("dom")
+    other = 1 - g
+    members = layout_of(groups, radices, g, d)
+
+    own_cells = pl.ds(pl.multiple_of(g * half, half), half)
+    other_cells = pl.ds(pl.multiple_of(other * half, half), half)
+    lev_load = pltpu.make_async_copy(levels, lev.at[g], local_sem.at[0])
+    xp_load = pltpu.make_async_copy(surplus.at[:, :, other_cells], xp, local_sem.at[1])
+    xb_load = pltpu.make_async_copy(surplus.at[:, :, own_cells], xb.at[pl.ds(g * local, local)], local_sem.at[2])
+    lev_load.start()
+    xp_load.start()
+    xb_load.start()
+
+    barrier = pltpu.get_barrier_semaphore()
+    count = 0
+    for n, mine, device in members:
+        for k in range(1, n):
+            pl.semaphore_signal(barrier, inc=1, device_id=device(lax.rem(mine + k, n)), device_id_type=MESH)
+            count += 1
+
+    lev_load.wait()
+    lev_eye = lax.broadcasted_iota(jnp.int32, (local, local), 0) == lax.broadcasted_iota(
+        jnp.int32, (local, local), 1
+    )
+    digits = digits_of(lax.broadcasted_iota(jnp.int32, (local, 128), 1))
+    keep = jnp.ones((local, 128), F32)
+    for axis in range(3):
+        lev_row = lev[g, axis:axis + 1, :].astype(F32)
+        lev_col = jnp.sum(jnp.where(lev_eye, lev_row, 0.0), axis=1, keepdims=True)
+        wide = jnp.broadcast_to(lev_col, (local, 128))
+        lev_out[axis] = wide
+        keep = jnp.where(wide >= digits[axis], keep, 0.0)
+    totals = count_dot(jnp.ones((local, local), F32), keep)
+    pos = count_dot(below(local, local, False), keep) + count_dot(totals, below(128, 128, True))
+    pos = jnp.where(keep > 0.0, pos, -1.0)
+    pos_far = pltpu.roll(pos, 64, 1)
+    own_count = jnp.sum(keep)
+
+    low = lax.broadcasted_iota(jnp.int32, (1, 128), 1) < subs
+    per = 128 // subs
+    pos_rows = [jnp.where(low, pos[i:i + 1], pos_far[i + 1:i + 2]) for i in range(0, local, per)]
+
+    xp_load.wait()
+    flat_p = xp.reshape(local * subs, half)
+    for i in range(0, local * subs, 256):
+        x = flat_p[i:i + 256, :]
+        hi = x.astype(jnp.bfloat16)
+        left = x - hi.astype(F32)
+        mid = left.astype(jnp.bfloat16)
+        xs[i:i + 256, 0:half] = hi
+        xs[i:i + 256, half:2 * half] = mid
+        xs[i:i + 256, 2 * half:] = (left - mid.astype(F32)).astype(jnp.bfloat16)
+
+    pl.semaphore_wait(barrier, count)
+    lev_copy = pltpu.make_async_remote_copy(
+        src_ref=lev.at[g], dst_ref=lev.at[g], send_sem=lev_sem.at[0], recv_sem=lev_sem.at[1],
+        device_id=(other, d), device_id_type=MESH,
+    )
+    lev_copy.start()
+
+    def x_copy(ch):
+        rows = pl.ds(pl.multiple_of(ch * STEP, STEP), STEP)
+        return pltpu.make_async_remote_copy(
+            src_ref=csend.at[rows], dst_ref=crecv.at[rows], send_sem=x_send.at[ch], recv_sem=x_recv.at[ch],
+            device_id=(other, d), device_id_type=MESH,
+        )
+
+    index = lax.broadcasted_iota(jnp.int32, (STEP, 128), 0).astype(F32)
+
+    def send_chunk(ch, carry):
+        want = index + (ch * STEP).astype(F32)
+        acc = jnp.zeros((STEP, 3 * half), F32)
+        for m in range(0, len(pos_rows), 2):
+            picks = [jnp.where(want == p, 1.0, 0.0).astype(jnp.bfloat16) for p in pos_rows[m:m + 2]]
+            acc += jnp.dot(
+                jnp.concatenate(picks, axis=1), xs[m * 128:m * 128 + 256, :], preferred_element_type=F32
+            )
+        rows = pl.ds(pl.multiple_of(ch * STEP, STEP), STEP)
+        csend[rows, :] = acc[:, :half] + acc[:, half:2 * half] + acc[:, 2 * half:]
+        x_copy(ch).start()
+        return carry
+
+    lax.fori_loop(0, chunks, send_chunk, 0)
+
+    xb_load.wait()
+    dig_wide = digits_of(lax.broadcasted_iota(jnp.int32, (subs, 128), 0))
+    for i in range(local):
+        own = (
+            (lev_out[0, i:i + 1, :] >= dig_wide[0])
+            & (lev_out[1, i:i + 1, :] >= dig_wide[1])
+            & (lev_out[2, i:i + 1, :] >= dig_wide[2])
+        )
+        for c in range(0, half, 128):
+            xp[i, :, c:c + 128] = jnp.where(own, xp[i, :, c:c + 128], 0.0)
+            xb[g * local + i, :, c:c + 128] = jnp.where(own, xb[g * local + i, :, c:c + 128], 0.0)
+    flat = xb.reshape(grids * subs, half)
+
+    prod[...] = jnp.zeros_like(prod)
+
+    def own_gram(ch, carry):
+        total = jnp.zeros(prod.shape, F32)
+        for k in range(ROWS):
+            s = ch * ROWS + k
+            y = split3(jnp.concatenate(
+                [flat_p[pl.ds(s, local, stride=subs), :], flat[pl.ds(g * local * subs + s, local, stride=subs), :]],
+                axis=1,
+            ))
+            total += outer(y, y)
+        prod[...] += total
+        return carry
+
+    lax.fori_loop(0, subs // ROWS, own_gram, 0)
+    copies = spread_out(
+        members, 0, own_slots[0], o_send[0], o_recv[0], pack(folded(prod[...], local))
+    )
+
+    lev_copy.wait_recv()
+    digits = digits_of(lax.broadcasted_iota(jnp.int32, (subs, local), 0))
+    keep = jnp.ones((subs, local), F32)
+    for axis in range(3):
+        keep = jnp.where(lev[other, axis:axis + 1, :].astype(F32) >= digits[axis], keep, 0.0)
+    totals = count_dot(keep, jnp.ones((local, local), F32))
+    pos = count_dot(below(subs, subs, False), totals) + count_dot(keep, below(local, local, True))
+    pos = jnp.where(keep > 0.0, pos, -1.0)
+    fits_out[0, 0] = jnp.where(jnp.maximum(own_count, jnp.sum(keep)) <= float(cap), 1, 0)
+    for i in range(local):
+        posb[i * subs:(i + 1) * subs, :] = jnp.broadcast_to(pos[:, i:i + 1], (subs, 128))
+    xb[pl.ds(other * local, local)] = jnp.zeros((local, subs, half), F32)
+    lane = lax.broadcasted_iota(jnp.int32, (256, STEP), 1).astype(F32)
+
+    def place_chunk(ch, carry):
+        x_copy(ch).wait_recv()
+        rows = pl.ds(pl.multiple_of(ch * STEP, STEP), STEP)
+        x = crecv[rows, :]
+        hi = x.astype(jnp.bfloat16)
+        left = x - hi.astype(F32)
+        mid = left.astype(jnp.bfloat16)
+        parts = jnp.concatenate([hi, mid, (left - mid.astype(F32)).astype(jnp.bfloat16)], axis=1)
+        want = lane + (ch * STEP).astype(F32)
+        for i in range(0, local * subs, 256):
+            picks = jnp.where(want == posb[i:i + 256, :], 1.0, 0.0).astype(jnp.bfloat16)
+            y = jnp.dot(picks, parts, preferred_element_type=F32)
+            at = pl.ds(pl.multiple_of(other * local * subs + i, 256), 256)
+            flat[at, :] += y[:, :half] + y[:, half:2 * half] + y[:, 2 * half:]
+        return carry
+
+    lax.fori_loop(0, chunks - 1, place_chunk, 0)
+    gather_in(members, 0, own_slots[0], o_send[0], o_recv[0])
+    half_n = members[0][0] // groups
+    own_total = jnp.concatenate(
+        [total_of(own_slots[0], 0, half_n), total_of(own_slots[0], half_n, 2 * half_n)], axis=0
+    )
+    if stages > 1:
+        copies += spread_out(members, 1, own_slots[1], o_send[1], o_recv[1], own_total)
+    lax.fori_loop(chunks - 1, chunks, place_chunk, 0)
+
+    cross[...] = jnp.zeros_like(cross)
+
+    def cross_gram(ch, carry):
+        total = jnp.zeros(cross.shape, F32)
+        for k in range(0, ROWS, 2):
+            s = ch * ROWS + k
+            sides = []
+            for h in range(groups):
+                sides.append(split3(jnp.concatenate(
+                    [flat[pl.ds(h * local * subs + s + j, local, stride=subs), :] for j in range(2)], axis=1
+                )))
+            total += outer(sides[0], sides[1])
+        cross[...] += total
+        return carry
+
+    lax.fori_loop(0, subs // ROWS, cross_gram, 0)
+    value = pack(folded(cross[...], local))
+    for t in range(stages):
+        copies += spread_out(members, t, slots[t], s_send[t], s_recv[t], value)
+        if t + 1 < stages:
+            nxt = t + 1
+            if t > 0:
+                copies += spread_out(members, nxt, own_slots[nxt], o_send[nxt], o_recv[nxt], own_total)
+            gather_in(members, nxt, own_slots[nxt], o_send[nxt], o_recv[nxt])
+            own_total = total_of(own_slots[nxt], 0, members[nxt][0])
+        gather_in(members, t, slots[t], s_send[t], s_recv[t])
+        value = total_of(slots[t], 0, members[t][0])
+
+    upper = unpack(value, local)
+    square = jnp.concatenate([upper, jnp.zeros((128 - local, 128), F32)], axis=0)
+    lower = square.T[:local]
+    value = jnp.concatenate(
+        [
+            unpack(own_total[:8], local) + pltpu.roll(upper, local, 1),
+            lower + pltpu.roll(unpack(own_total[8:], local), local, 1),
+        ],
+        axis=0,
+    )
+    coef_wide, eye = solve(value, grids)
+    coef_out[...] = jnp.sum(jnp.where(eye, coef_wide, 0.0), axis=0, keepdims=True)[:, :grids]
+
+    piece = subs // PIECES
+
+    def c_copy(slot, p):
+        block = cbuf.at[slot, pl.ds(p * piece, piece)]
+        return pltpu.make_async_remote_copy(
+            src_ref=block, dst_ref=block, send_sem=c_send.at[p], recv_sem=c_recv.at[p],
+            device_id=(other, d), device_id_type=MESH,
+        )
+
+    for p in range(PIECES):
+        acc = jnp.zeros((piece, half), F32)
+        for i in range(grids):
+            acc += coef_wide[i:i + 1, 0:1] * xb[i, p * piece:(p + 1) * piece]
+        cbuf[g, p * piece:(p + 1) * piece] = acc
+        c_copy(g, p).start()
+    for p in range(PIECES):
+        c_copy(other, p).wait_recv()
+    for h in range(groups):
+        comb_out[:, h * half:(h + 1) * half] = cbuf[h]
+
+    for copy in copies:
+        copy.wait_send()
+    lev_copy.wait_send()
+    for ch in range(chunks):
+        x_copy(ch).wait_send()
+    for p in range(PIECES):
+        c_copy(g, p).wait_send()
+
+
 def spread(combined, coef, lev, updated, coef_out, block, sems):
     local, subs, cells = updated.shape
     coef_out[...] = coef[...]
@@ -277,22 +631,21 @@
         copy.wait()
 
 
-def shards(groups, domains, surplus, levels):
+def dense_call(groups, radices, surplus, levels, identity):
     local, subs, cells = surplus.shape
     grids = groups * local
     half = cells // groups
-    radices = radices_of(domains)
     sizes = [groups * r if t == 0 else r for t, r in enumerate(radices)]
     dma = pltpu.SemaphoreType.DMA
     chunks = subs // ROWS
-    combined, coefficients, lev_wide = pl.pallas_call(
+    return pl.pallas_call(
         functools.partial(kernel, groups, radices, local, subs),
         out_shape=(
             jax.ShapeDtypeStruct((subs, cells), F32),
             jax.ShapeDtypeStruct((1, grids), F32),
             jax.ShapeDtypeStruct((3, local, 128), F32),
         ),
-        in_specs=[pl.BlockSpec(memory_space=pl.ANY), pl.BlockSpec(memory_space=pltpu.VMEM)],
+        in_specs=[pl.BlockSpec(memory_space=pltpu.HBM), pl.BlockSpec(memory_space=pltpu.VMEM)],
         out_specs=tuple(pl.BlockSpec(memory_space=pltpu.VMEM) for _ in range(3)),
         scratch_shapes=[
             pltpu.VMEM((grids, subs, half), F32),
@@ -306,8 +659,68 @@
         + [pltpu.VMEM((n, grids // 2, 128), F32) for n in sizes]
         + [dma((n,)) for n in sizes]
         + [dma((n,)) for n in sizes],
-        compiler_params=pltpu.CompilerParams(collective_id=0, has_side_effects=True),
-    )(surplus, levels.T)
+        compiler_params=pltpu.CompilerParams(
+            collective_id=identity, has_side_effects=True, vmem_limit_bytes=VMEM_BYTES
+        ),
+    )(surplus, levels)
+
+
+def sparse_call(groups, radices, surplus, levels, identity):
+    local, subs, cells = surplus.shape
+    grids = groups * local
+    half = cells // groups
+    cap = local * subs // 3 // STEP * STEP
+    sizes = [groups * r if t == 0 else r for t, r in enumerate(radices)]
+    dma = pltpu.SemaphoreType.DMA
+    return pl.pallas_call(
+        functools.partial(sparse_kernel, groups, radices, local, subs, cap),
+        out_shape=(
+            jax.ShapeDtypeStruct((subs, cells), F32),
+            jax.ShapeDtypeStruct((1, grids), F32),
+            jax.ShapeDtypeStruct((3, local, 128), F32),
+            jax.ShapeDtypeStruct((1, 1), jnp.int32),
+        ),
+        in_specs=[pl.BlockSpec(memory_space=pltpu.HBM), pl.BlockSpec(memory_space=pltpu.HBM)],
+        out_specs=tuple(pl.BlockSpec(memory_space=pltpu.VMEM) for _ in range(3))
+        + (pl.BlockSpec(memory_space=pltpu.SMEM),),
+        scratch_shapes=[
+            pltpu.VMEM((grids, subs, half), F32),
+            pltpu.VMEM((local, subs, half), F32),
+            pltpu.VMEM((local * subs, 3 * half), jnp.bfloat16),
+            pltpu.VMEM((cap, half), F32),
+            pltpu.VMEM((cap, half), F32),
+            pltpu.VMEM((local * subs, 128), F32),
+            pltpu.VMEM((groups, 3, local), jnp.int32),
+            pltpu.VMEM((3, grids, 128), F32),
+            pltpu.VMEM((3 * local, 3 * local), F32),
+            pltpu.VMEM((3 * local, 3 * local), F32),
+            pltpu.VMEM((groups, subs, half), F32),
+            dma((3,)), dma((2,)), dma((cap // STEP,)), dma((cap // STEP,)), dma((PIECES,)), dma((PIECES,)),
+        ]
+        + [pltpu.VMEM((n, 8, 128), F32) for n in sizes]
+        + [dma((n,)) for n in sizes]
+        + [dma((n,)) for n in sizes]
+        + [pltpu.VMEM((n, 8 if t == 0 else 16, 128), F32) for t, n in enumerate(sizes)]
+        + [dma((n,)) for n in sizes]
+        + [dma((n,)) for n in sizes],
+        compiler_params=pltpu.CompilerParams(
+            collective_id=identity, has_side_effects=True, vmem_limit_bytes=VMEM_BYTES
+        ),
+    )(surplus, levels)
+
+
+def shards(groups, domains, surplus, levels):
+    local, subs, cells = surplus.shape
+    grids = groups * local
+    radices = radices_of(domains)
+    flipped = levels.T
+    *found, fits = sparse_call(groups, radices, surplus, flipped, 0)
+    combined, coefficients, lev_wide = lax.cond(
+        fits[0, 0] == 1,
+        lambda *kept: tuple(kept[2:]),
+        lambda *kept: tuple(dense_call(groups, radices, kept[0], kept[1], 1)),
+        surplus, flipped, *found,
+    )
     updated, coefficients = pl.pallas_call(
         spread,
         out_shape=(
@@ -316,7 +729,8 @@
         ),
         in_specs=[pl.BlockSpec(memory_space=pltpu.VMEM)] * 3,
         out_specs=(pl.BlockSpec(memory_space=pl.ANY), pl.BlockSpec(memory_space=pltpu.VMEM)),
-        scratch_shapes=[pltpu.VMEM((local, subs, cells), F32), dma((-(-local // SPREAD),))],
+        scratch_shapes=[pltpu.VMEM((local, subs, cells), F32), pltpu.SemaphoreType.DMA((-(-local // SPREAD),))],
+        compiler_params=pltpu.CompilerParams(vmem_limit_bytes=VMEM_BYTES),
     )(combined, coefficients, lev_wide)
     return (updated, coefficients.reshape(grids))
 

time: 41.6 us -> 32.6 us (0.78)
  Pallas kernels: 40.8 us -> 31.1 us
  between operations: 0.64 us -> 1.37 us
    pallas_call x1, Pallas kernels: 38.2 us -> 29.3 us  [sparse_call(): pl.pallas_call(functools.partial(sparse_kernel, groups, radices, local, s...]
    pallas_call x1, Pallas kernels: 2.59 us -> 1.74 us  [shards(): pl.pallas_call(spread, out_shape=(jax.ShapeDtypeStruct((local, subs, cell...]
where the time goes in v1:
time: 32.6 us; the launch traced here: 32.5 us
  Pallas kernels  31.1 us (95%)
  between operations  1.37 us (4%)
    pallas_call x1, Pallas kernels, sparse_call(): pl.pallas_call(functools.partial(sparse_kernel, groups, radices, local, s...  29.3 us
    pallas_call x1, Pallas kernels, shards(): pl.pallas_call(spread, out_shape=(jax.ShapeDtypeStruct((local, subs, cell...  1.74 us

profile of v1, /device:TPU:0, one launch (start us, length us, event | category | flops | bytes accessed | tf_op | source)
XLA Modules:
  0.0 32.5 jit_solution(5713325473346671966)
XLA Ops:
  0.6 0.0 copy-start
  0.6 0.0 copy-start.1
  0.6 29.3 %shard_map.41 = (f32[64,256]{1,0:T(8,128)S(1)}, f32[1,48]{1,0:T(1,128)S(1)}, f32[3,24,128]{2,1,0:T(8,128)S(1)}, s32[1,1]{1,0:T(1,128)}) custom-call(f32[24,64,256]{2,1,0:T(8,128)} %surplus.1, s32[3,24]{1,0:T(4,128)} %bitcast.3), custom_call_target="tpu_custom_call" | custom-call | tf_op jit(solution)/shard_map/pallas_call | solution.py:675
  30.7 0.0 copy-done
  30.7 0.0 copy-done.1
  30.7 1.7 %shard_map.42 = (f32[24,64,256]{2,1,0:T(8,128)}, f32[1,48]{1,0:T(1,128)}) custom-call(f32[64,256]{1,0:T(8,128)S(1)} %get-tuple-element.27.combined, f32[1,48]{1,0:T(1,128)S(1)} %get-tuple-element.28.coef, f32[3,24,128]{2,1,0:T(8,128)S(1)} %get-tuple-element.29.lev), custom_call_target="tpu_custom_call" | custom-call | tf_op jit(solution)/shard_map/pallas_call | solution.py:724
  (1 shorter events, 0.0 us)
Async XLA Ops:
  0.6 30.0 %copy-start = (f32[24,64,256]{2,1,0:T(8,128)S(1)}, f32[24,64,256]{2,1,0:T(8,128)}, u32[]{:S(2)}) copy-start(f32[24,64,256]{2,1,0:T(8,128)} %surplus.1) | copy-start | bytes 4718596
  0.6 30.0 %copy-start.1 = (s32[24,3]{0,1:T(4,128)S(1)}, s32[24,3]{0,1:T(4,128)}, u32[]{:S(2)}) copy-start(s32[24,3]{0,1:T(4,128)} %param.5) | copy-start | bytes 868

commit v2 on v1

--- a/solution.py
+++ b/solution.py
@@ -14,7 +14,9 @@
 SPREAD = 4
 SLOT = 32
 STEP = 128
-VMEM_BYTES = 24 * 1024 * 1024
+EARLY = 1
+BAND = 384
+VMEM_BYTES = 32 * 1024 * 1024
 F32 = jnp.float32
 
 
@@ -261,6 +263,13 @@
             c_copy(g, k, p).wait_send()
 
 
+def split3_rows(x):
+    hi = x.astype(jnp.bfloat16).astype(F32)
+    rest = x - hi
+    mid = rest.astype(jnp.bfloat16).astype(F32)
+    return jnp.concatenate([hi, mid, rest - mid], axis=0).astype(jnp.bfloat16)
+
+
 def layout_of(groups, radices, g, d):
     members = []
     stride = 1
@@ -376,28 +385,52 @@
     return jnp.broadcast_to(coef, (grids, 128)), eye
 
 
+def parts_of(x):
+    hi = x.astype(jnp.bfloat16)
+    left = x - hi.astype(F32)
+    mid = left.astype(jnp.bfloat16)
+    return hi, mid, (left - mid.astype(F32)).astype(jnp.bfloat16)
+
+
+def places_of(keep, across):
+    n, m = keep.shape
+    if across:
+        totals = count_dot(jnp.ones((n, n), F32), keep)
+        pos = count_dot(below(n, n, False), keep) + count_dot(totals, below(m, m, True))
+    else:
+        totals = count_dot(keep, jnp.ones((m, m), F32))
+        pos = count_dot(below(n, n, False), totals) + count_dot(keep, below(m, m, True))
+    return jnp.where(keep > 0.0, pos, -1.0)
+
+
 def sparse_kernel(groups, radices, local, subs, cap, surplus, levels, comb_out, coef_out, lev_out, fits_out, *scratch):
     stages = len(radices)
-    (xb, xp, xs, csend, crecv, posb, lev, lbc, prod, cross, cbuf, local_sem, lev_sem, x_send, x_recv, c_send,
-     c_recv) = scratch[:17]
-    rest = [scratch[17 + m * stages:17 + (m + 1) * stages] for m in range(6)]
+    (xh, xm, xs, ym, pm, csend, crecv, posm, lev, prod, cbuf, local_sem, m_sem, lev_sem, x_send,
+     x_recv) = scratch[:16]
+    rest = [scratch[16 + m * stages:16 + (m + 1) * stages] for m in range(6)]
     slots, s_send, s_recv, own_slots, o_send, o_recv = rest
     grids = groups * local
-    half = xb.shape[-1]
+    half = xh.shape[-1]
+    rows_all = local * subs
     chunks = cap // STEP
+    bf16 = jnp.bfloat16
     g = lax.axis_index("grp")
     d = lax.axis_index("dom")
     other = 1 - g
     members = layout_of(groups, radices, g, d)
 
-    own_cells = pl.ds(pl.multiple_of(g * half, half), half)
-    other_cells = pl.ds(pl.multiple_of(other * half, half), half)
-    lev_load = pltpu.make_async_copy(levels, lev.at[g], local_sem.at[0])
-    xp_load = pltpu.make_async_copy(surplus.at[:, :, other_cells], xp, local_sem.at[1])
-    xb_load = pltpu.make_async_copy(surplus.at[:, :, own_cells], xb.at[pl.ds(g * local, local)], local_sem.at[2])
+    cells = [pl.ds(pl.multiple_of(h * half, half), half) for h in (other, g)]
+    lev_load = pltpu.make_async_copy(levels, lev.at[g], local_sem.at[2])
     lev_load.start()
-    xp_load.start()
-    xb_load.start()
+    loads = [pltpu.make_async_copy(surplus.at[:, :, cells[h]], xh.at[h], local_sem.at[h]) for h in range(2)]
+    for load in loads:
+        load.start()
+    turns = [
+        pltpu.make_async_copy(surplus.at[i, :, cells[h]], xm.at[h, :, i, :], m_sem.at[h, i])
+        for i in range(local) for h in range(2)
+    ]
+    for turn in turns:
+        turn.start()
 
     barrier = pltpu.get_barrier_semaphore()
     count = 0
@@ -406,39 +439,41 @@
             pl.semaphore_signal(barrier, inc=1, device_id=device(lax.rem(mine + k, n)), device_id_type=MESH)
             count += 1
 
+    def lev_wide(h):
+        eye = lax.broadcasted_iota(jnp.int32, (local, local), 0) == lax.broadcasted_iota(jnp.int32, (local, local), 1)
+        out = []
+        for axis in range(3):
+            lev_row = lev[h, axis:axis + 1, :].astype(F32)
+            lev_col = jnp.sum(jnp.where(eye, lev_row, 0.0), axis=1, keepdims=True)
+            out.append(jnp.broadcast_to(lev_col, (local, 128)))
+        return out
+
+    def kept_by(wide):
+        digits = digits_of(lax.broadcasted_iota(jnp.int32, (local, 128), 1))
+        keep = jnp.ones((local, 128), F32)
+        for axis in range(3):
+            keep = jnp.where(wide[axis] >= digits[axis], keep, 0.0)
+        return keep
+
     lev_load.wait()
-    lev_eye = lax.broadcasted_iota(jnp.int32, (local, local), 0) == lax.broadcasted_iota(
-        jnp.int32, (local, local), 1
-    )
-    digits = digits_of(lax.broadcasted_iota(jnp.int32, (local, 128), 1))
-    keep = jnp.ones((local, 128), F32)
+    wide = lev_wide(g)
     for axis in range(3):
-        lev_row = lev[g, axis:axis + 1, :].astype(F32)
-        lev_col = jnp.sum(jnp.where(lev_eye, lev_row, 0.0), axis=1, keepdims=True)
-        wide = jnp.broadcast_to(lev_col, (local, 128))
-        lev_out[axis] = wide
-        keep = jnp.where(wide >= digits[axis], keep, 0.0)
-    totals = count_dot(jnp.ones((local, local), F32), keep)
-    pos = count_dot(below(local, local, False), keep) + count_dot(totals, below(128, 128, True))
-    pos = jnp.where(keep > 0.0, pos, -1.0)
+        lev_out[axis] = wide[axis]
+    keep = kept_by(wide)
+    own_count = jnp.sum(keep)
+    pos = places_of(keep, True)
     pos_far = pltpu.roll(pos, 64, 1)
-    own_count = jnp.sum(keep)
-
     low = lax.broadcasted_iota(jnp.int32, (1, 128), 1) < subs
-    per = 128 // subs
-    pos_rows = [jnp.where(low, pos[i:i + 1], pos_far[i + 1:i + 2]) for i in range(0, local, per)]
-
-    xp_load.wait()
-    flat_p = xp.reshape(local * subs, half)
-    for i in range(0, local * subs, 256):
-        x = flat_p[i:i + 256, :]
-        hi = x.astype(jnp.bfloat16)
-        left = x - hi.astype(F32)
-        mid = left.astype(jnp.bfloat16)
-        xs[i:i + 256, 0:half] = hi
-        xs[i:i + 256, half:2 * half] = mid
-        xs[i:i + 256, 2 * half:] = (left - mid.astype(F32)).astype(jnp.bfloat16)
-
+    pos_rows = [jnp.where(low, pos[i:i + 1], pos_far[i + 1:i + 2]) for i in range(0, local, 128 // subs)]
+
+    def split_half(h):
+        flat = xh.at[h].reshape(rows_all, half)
+        for i in range(0, rows_all, 256):
+            for m, part in enumerate(parts_of(flat[i:i + 256, :])):
+                xs[h, i:i + 256, m * half:(m + 1) * half] = part
+
+    loads[0].wait()
+    split_half(0)
     pl.semaphore_wait(barrier, count)
     lev_copy = pltpu.make_async_remote_copy(
         src_ref=lev.at[g], dst_ref=lev.at[g], send_sem=lev_sem.at[0], recv_sem=lev_sem.at[1],
@@ -446,127 +481,138 @@
     )
     lev_copy.start()
 
-    def x_copy(ch):
+    def x_copy(h, ch):
         rows = pl.ds(pl.multiple_of(ch * STEP, STEP), STEP)
         return pltpu.make_async_remote_copy(
-            src_ref=csend.at[rows], dst_ref=crecv.at[rows], send_sem=x_send.at[ch], recv_sem=x_recv.at[ch],
+            src_ref=csend.at[h, rows], dst_ref=crecv.at[h, rows], send_sem=x_send.at[h, ch], recv_sem=x_recv.at[h, ch],
             device_id=(other, d), device_id_type=MESH,
         )
 
     index = lax.broadcasted_iota(jnp.int32, (STEP, 128), 0).astype(F32)
 
-    def send_chunk(ch, carry):
+    def gather_chunk(h, ch):
         want = index + (ch * STEP).astype(F32)
         acc = jnp.zeros((STEP, 3 * half), F32)
         for m in range(0, len(pos_rows), 2):
-            picks = [jnp.where(want == p, 1.0, 0.0).astype(jnp.bfloat16) for p in pos_rows[m:m + 2]]
+            picks = [jnp.where(want == p, 1.0, 0.0).astype(bf16) for p in pos_rows[m:m + 2]]
             acc += jnp.dot(
-                jnp.concatenate(picks, axis=1), xs[m * 128:m * 128 + 256, :], preferred_element_type=F32
+                jnp.concatenate(picks, axis=1), xs[h, m * 128:m * 128 + 256, :], preferred_element_type=F32
             )
         rows = pl.ds(pl.multiple_of(ch * STEP, STEP), STEP)
-        csend[rows, :] = acc[:, :half] + acc[:, half:2 * half] + acc[:, 2 * half:]
-        x_copy(ch).start()
+        csend[h, rows, :] = acc[:, :half] + acc[:, half:2 * half] + acc[:, 2 * half:]
+
+    def send_chunk(h, ch, carry):
+        gather_chunk(h, ch)
+        x_copy(h, ch).start()
         return carry
 
-    lax.fori_loop(0, chunks, send_chunk, 0)
-
-    xb_load.wait()
-    dig_wide = digits_of(lax.broadcasted_iota(jnp.int32, (subs, 128), 0))
-    for i in range(local):
-        own = (
-            (lev_out[0, i:i + 1, :] >= dig_wide[0])
-            & (lev_out[1, i:i + 1, :] >= dig_wide[1])
-            & (lev_out[2, i:i + 1, :] >= dig_wide[2])
-        )
-        for c in range(0, half, 128):
-            xp[i, :, c:c + 128] = jnp.where(own, xp[i, :, c:c + 128], 0.0)
-            xb[g * local + i, :, c:c + 128] = jnp.where(own, xb[g * local + i, :, c:c + 128], 0.0)
-    flat = xb.reshape(grids * subs, half)
-
+    def hold_chunk(h, ch, carry):
+        gather_chunk(h, ch)
+        return carry
+
+    lax.fori_loop(0, chunks, functools.partial(send_chunk, 0), 0)
+    loads[1].wait()
+    split_half(1)
+    lax.fori_loop(0, EARLY, functools.partial(send_chunk, 1), 0)
+
+    for turn in turns:
+        turn.wait()
     prod[...] = jnp.zeros_like(prod)
 
     def own_gram(ch, carry):
         total = jnp.zeros(prod.shape, F32)
         for k in range(ROWS):
             s = ch * ROWS + k
-            y = split3(jnp.concatenate(
-                [flat_p[pl.ds(s, local, stride=subs), :], flat[pl.ds(g * local * subs + s, local, stride=subs), :]],
-                axis=1,
-            ))
+            own = (
+                (lev_out[0] >= (s // 16).astype(F32))
+                & (lev_out[1] >= lax.rem(s // 4, 4).astype(F32))
+                & (lev_out[2] >= float(k % 4))
+            )
+            own = jnp.concatenate([own] * (half // 128), axis=1) if half > 128 else own
+            pair = [jnp.where(own, xm[h, s], 0.0) for h in range(2)]
+            for h in range(2):
+                xm[h, s] = pair[h]
+            y = split3_rows(jnp.concatenate(pair, axis=1))
+            ym[s] = y[:, half:]
             total += outer(y, y)
         prod[...] += total
         return carry
 
     lax.fori_loop(0, subs // ROWS, own_gram, 0)
-    copies = spread_out(
-        members, 0, own_slots[0], o_send[0], o_recv[0], pack(folded(prod[...], local))
-    )
+    copies = spread_out(members, 0, own_slots[0], o_send[0], o_recv[0], pack(folded(prod[...], local)))
+    lax.fori_loop(EARLY, chunks, functools.partial(hold_chunk, 1), 0)
 
     lev_copy.wait_recv()
-    digits = digits_of(lax.broadcasted_iota(jnp.int32, (subs, local), 0))
-    keep = jnp.ones((subs, local), F32)
-    for axis in range(3):
-        keep = jnp.where(lev[other, axis:axis + 1, :].astype(F32) >= digits[axis], keep, 0.0)
-    totals = count_dot(keep, jnp.ones((local, local), F32))
-    pos = count_dot(below(subs, subs, False), totals) + count_dot(keep, below(local, local, True))
-    pos = jnp.where(keep > 0.0, pos, -1.0)
+    keep = kept_by(lev_wide(other))
     fits_out[0, 0] = jnp.where(jnp.maximum(own_count, jnp.sum(keep)) <= float(cap), 1, 0)
-    for i in range(local):
-        posb[i * subs:(i + 1) * subs, :] = jnp.broadcast_to(pos[:, i:i + 1], (subs, 128))
-    xb[pl.ds(other * local, local)] = jnp.zeros((local, subs, half), F32)
-    lane = lax.broadcasted_iota(jnp.int32, (256, STEP), 1).astype(F32)
-
-    def place_chunk(ch, carry):
-        x_copy(ch).wait_recv()
-        rows = pl.ds(pl.multiple_of(ch * STEP, STEP), STEP)
-        x = crecv[rows, :]
-        hi = x.astype(jnp.bfloat16)
-        left = x - hi.astype(F32)
-        mid = left.astype(jnp.bfloat16)
-        parts = jnp.concatenate([hi, mid, (left - mid.astype(F32)).astype(jnp.bfloat16)], axis=1)
-        want = lane + (ch * STEP).astype(F32)
-        for i in range(0, local * subs, 256):
-            picks = jnp.where(want == posb[i:i + 256, :], 1.0, 0.0).astype(jnp.bfloat16)
-            y = jnp.dot(picks, parts, preferred_element_type=F32)
-            at = pl.ds(pl.multiple_of(other * local * subs + i, 256), 256)
-            flat[at, :] += y[:, :half] + y[:, half:2 * half] + y[:, 2 * half:]
-        return carry
-
-    lax.fori_loop(0, chunks - 1, place_chunk, 0)
-    gather_in(members, 0, own_slots[0], o_send[0], o_recv[0])
-    half_n = members[0][0] // groups
-    own_total = jnp.concatenate(
-        [total_of(own_slots[0], 0, half_n), total_of(own_slots[0], half_n, 2 * half_n)], axis=0
-    )
-    if stages > 1:
-        copies += spread_out(members, 1, own_slots[1], o_send[1], o_recv[1], own_total)
-    lax.fori_loop(chunks - 1, chunks, place_chunk, 0)
-
-    cross[...] = jnp.zeros_like(cross)
-
-    def cross_gram(ch, carry):
-        total = jnp.zeros(cross.shape, F32)
-        for k in range(0, ROWS, 2):
-            s = ch * ROWS + k
-            sides = []
-            for h in range(groups):
-                sides.append(split3(jnp.concatenate(
-                    [flat[pl.ds(h * local * subs + s + j, local, stride=subs), :] for j in range(2)], axis=1
-                )))
-            total += outer(sides[0], sides[1])
-        cross[...] += total
-        return carry
-
-    lax.fori_loop(0, subs // ROWS, cross_gram, 0)
-    value = pack(folded(cross[...], local))
+    pos = places_of(keep, True)
+    for s in range(subs):
+        posm[s * local:(s + 1) * local, :] = jnp.broadcast_to(pos[:, s:s + 1], (local, 128))
+
+    def parts_at(h, first):
+        return jnp.concatenate(parts_of(crecv[h, first:first + 256, :]), axis=1)
+
+    def placed(where, first, parts, n):
+        lane = lax.broadcasted_iota(jnp.int32, (n, 128), 1).astype(F32) + float(first)
+        picks = [jnp.where(where == lane + float(c), 1.0, 0.0).astype(bf16) for c in range(0, 256, 128)]
+        y = jnp.dot(jnp.concatenate(picks, axis=1), parts, preferred_element_type=F32)
+        return y[:, :half] + y[:, half:2 * half] + y[:, 2 * half:]
+
+    def arrive(h, first):
+        for ch in range(first // STEP, (first + 256) // STEP):
+            x_copy(h, ch).wait_recv()
+
+    last = cap - 256
+    for first in range(0, last, 256):
+        arrive(0, first)
+        parts = parts_at(0, first)
+
+        for at in range(0, rows_all, BAND):
+            y = placed(posm[at:at + BAND, :], first, parts, BAND)
+            pm[1, at:at + BAND, :] = y if first == 0 else pm[1, at:at + BAND, :] + y
+
+    arrive(0, last)
+    parts = parts_at(0, last)
+    total = jnp.zeros((3 * local, 3 * local), F32)
+    for at in range(0, rows_all, BAND):
+        y = placed(posm[at:at + BAND, :], last, parts, BAND)
+        if last > 0:
+            y = y + pm[1, at:at + BAND, :]
+        pm[1, at:at + BAND, :] = y
+        for k in range(0, BAND // local, 2):
+            s = at // local + k
+            theirs = split3_rows(
+                jnp.concatenate([y[(k + j) * local:(k + j + 1) * local] for j in range(2)], axis=1)
+            )
+            ours = jnp.concatenate([ym[s], ym[s + 1]], axis=1)
+            total += outer(jnp.where(g == 0, ours, theirs), jnp.where(g == 0, theirs, ours))
+
+    def finish_late():
+        for first in range(0, cap, 256):
+            arrive(1, first)
+            parts = parts_at(1, first)
+            for at in range(0, rows_all, BAND):
+                y = placed(posm[at:at + BAND, :], first, parts, BAND)
+                pm[0, at:at + BAND, :] = y if first == 0 else pm[0, at:at + BAND, :] + y
+
+    value = pack(folded(total, local))
     for t in range(stages):
         copies += spread_out(members, t, slots[t], s_send[t], s_recv[t], value)
+        if t == 0:
+            for ch in range(EARLY, chunks):
+                x_copy(1, ch).start()
+        gather_in(members, t, own_slots[t], o_send[t], o_recv[t])
+        n = members[t][0]
+        if t == 0:
+            own_total = jnp.concatenate(
+                [total_of(own_slots[0], 0, n // 2), total_of(own_slots[0], n // 2, n)], axis=0
+            )
+        else:
+            own_total = total_of(own_slots[t], 0, n)
         if t + 1 < stages:
-            nxt = t + 1
-            if t > 0:
-                copies += spread_out(members, nxt, own_slots[nxt], o_send[nxt], o_recv[nxt], own_total)
-            gather_in(members, nxt, own_slots[nxt], o_send[nxt], o_recv[nxt])
-            own_total = total_of(own_slots[nxt], 0, members[nxt][0])
+            copies += spread_out(members, t + 1, own_slots[t + 1], o_send[t + 1], o_recv[t + 1], own_total)
+        else:
+            finish_late()
         gather_in(members, t, slots[t], s_send[t], s_recv[t])
         value = total_of(slots[t], 0, members[t][0])
 
@@ -583,33 +629,26 @@
     coef_wide, eye = solve(value, grids)
     coef_out[...] = jnp.sum(jnp.where(eye, coef_wide, 0.0), axis=0, keepdims=True)[:, :grids]
 
-    piece = subs // PIECES
-
-    def c_copy(slot, p):
-        block = cbuf.at[slot, pl.ds(p * piece, piece)]
-        return pltpu.make_async_remote_copy(
-            src_ref=block, dst_ref=block, send_sem=c_send.at[p], recv_sem=c_recv.at[p],
-            device_id=(other, d), device_id_type=MESH,
-        )
-
-    for p in range(PIECES):
-        acc = jnp.zeros((piece, half), F32)
-        for i in range(grids):
-            acc += coef_wide[i:i + 1, 0:1] * xb[i, p * piece:(p + 1) * piece]
-        cbuf[g, p * piece:(p + 1) * piece] = acc
-        c_copy(g, p).start()
-    for p in range(PIECES):
-        c_copy(other, p).wait_recv()
+    ours = jnp.where(g == 0, coef_wide[:local], coef_wide[local:])
+    theirs = jnp.where(g == 0, coef_wide[local:], coef_wide[:local])
+    if half > 128:
+        ours, theirs = [jnp.concatenate([w] * (half // 128), axis=1) for w in (ours, theirs)]
+    for h, slot in ((0, other), (1, g)):
+        for first in range(0, subs, 8):
+            at = first * local
+            acc = xm[h, first:first + 8] * ours[None] + (
+                pm[h, at:at + 8 * local, :].reshape(8, local, half) * theirs[None]
+            )
+            cbuf[slot, first:first + 8] = jnp.sum(acc, axis=1)
     for h in range(groups):
         comb_out[:, h * half:(h + 1) * half] = cbuf[h]
 
     for copy in copies:
         copy.wait_send()
     lev_copy.wait_send()
-    for ch in range(chunks):
-        x_copy(ch).wait_send()
-    for p in range(PIECES):
-        c_copy(g, p).wait_send()
+    for h in range(2):
+        for ch in range(chunks):
+            x_copy(h, ch).wait_send()
 
 
 def spread(combined, coef, lev, updated, coef_out, block, sems):
@@ -669,7 +708,8 @@
     local, subs, cells = surplus.shape
     grids = groups * local
     half = cells // groups
-    cap = local * subs // 3 // STEP * STEP
+    cap = local * subs // 3 // 256 * 256
+    chunks = cap // STEP
     sizes = [groups * r if t == 0 else r for t, r in enumerate(radices)]
     dma = pltpu.SemaphoreType.DMA
     return pl.pallas_call(
@@ -684,18 +724,18 @@
         out_specs=tuple(pl.BlockSpec(memory_space=pltpu.VMEM) for _ in range(3))
         + (pl.BlockSpec(memory_space=pltpu.SMEM),),
         scratch_shapes=[
-            pltpu.VMEM((grids, subs, half), F32),
-            pltpu.VMEM((local, subs, half), F32),
-            pltpu.VMEM((local * subs, 3 * half), jnp.bfloat16),
-            pltpu.VMEM((cap, half), F32),
-            pltpu.VMEM((cap, half), F32),
+            pltpu.VMEM((2, local, subs, half), F32),
+            pltpu.VMEM((2, subs, local, half), F32),
+            pltpu.VMEM((2, local * subs, 3 * half), jnp.bfloat16),
+            pltpu.VMEM((subs, 3 * local, half), jnp.bfloat16),
+            pltpu.VMEM((2, local * subs, half), F32),
+            pltpu.VMEM((2, cap, half), F32),
+            pltpu.VMEM((2, cap, half), F32),
             pltpu.VMEM((local * subs, 128), F32),
             pltpu.VMEM((groups, 3, local), jnp.int32),
-            pltpu.VMEM((3, grids, 128), F32),
-            pltpu.VMEM((3 * local, 3 * local), F32),
             pltpu.VMEM((3 * local, 3 * local), F32),
             pltpu.VMEM((groups, subs, half), F32),
-            dma((3,)), dma((2,)), dma((cap // STEP,)), dma((cap // STEP,)), dma((PIECES,)), dma((PIECES,)),
+            dma((3,)), dma((2, local)), dma((2,)), dma((2, chunks)), dma((2, chunks)),
         ]
         + [pltpu.VMEM((n, 8, 128), F32) for n in sizes]
         + [dma((n,)) for n in sizes]

time: 32.6 us -> 28.9 us (0.89)
  Pallas kernels: 31.1 us -> 27.4 us
    pallas_call x1, Pallas kernels: 29.3 us -> 25.6 us  [sparse_call(): pl.pallas_call(functools.partial(sparse_kernel, groups, radices, local, s...]
where the time goes in v2:
time: 28.9 us; the launch traced here: 28.8 us
  Pallas kernels  27.4 us (95%)
  between operations  1.37 us (5%)
    pallas_call x1, Pallas kernels, sparse_call(): pl.pallas_call(functools.partial(sparse_kernel, groups, radices, local, s...  25.6 us
    pallas_call x1, Pallas kernels, shards(): pl.pallas_call(spread, out_shape=(jax.ShapeDtypeStruct((local, subs, cell...  1.74 us

profile of v2, /device:TPU:0, one launch (start us, length us, event | category | flops | bytes accessed | tf_op | source)
XLA Modules:
  0.0 28.8 jit_solution(5214810707598363910)
XLA Ops:
  0.6 0.0 copy-start
  0.6 0.0 copy-start.1
  0.6 25.6 %shard_map.41 = (f32[64,256]{1,0:T(8,128)S(1)}, f32[1,48]{1,0:T(1,128)S(1)}, f32[3,24,128]{2,1,0:T(8,128)S(1)}, s32[1,1]{1,0:T(1,128)}) custom-call(f32[24,64,256]{2,1,0:T(8,128)} %surplus.1, s32[3,24]{1,0:T(4,128)} %bitcast.3), custom_call_target="tpu_custom_call" | custom-call | tf_op jit(solution)/shard_map/pallas_call | solution.py:715
  27.0 0.0 copy-done
  27.0 0.0 copy-done.1
  27.0 1.7 %shard_map.42 = (f32[24,64,256]{2,1,0:T(8,128)}, f32[1,48]{1,0:T(1,128)}) custom-call(f32[64,256]{1,0:T(8,128)S(1)} %get-tuple-element.27.combined, f32[1,48]{1,0:T(1,128)S(1)} %get-tuple-element.28.coef, f32[3,24,128]{2,1,0:T(8,128)S(1)} %get-tuple-element.29.lev), custom_call_target="tpu_custom_call" | custom-call | tf_op jit(solution)/shard_map/pallas_call | solution.py:764
  (1 shorter events, 0.0 us)
Async XLA Ops:
  0.6 26.4 %copy-start = (f32[24,64,256]{2,1,0:T(8,128)S(1)}, f32[24,64,256]{2,1,0:T(8,128)}, u32[]{:S(2)}) copy-start(f32[24,64,256]{2,1,0:T(8,128)} %surplus.1) | copy-start | bytes 4718596
  0.6 26.4 %copy-start.1 = (s32[24,3]{0,1:T(4,128)S(1)}, s32[24,3]{0,1:T(4,128)}, u32[]{:S(2)}) copy-start(s32[24,3]{0,1:T(4,128)} %param.5) | copy-start | bytes 868

commit v3 on v2

--- a/solution.py
+++ b/solution.py
@@ -14,7 +14,7 @@
 SPREAD = 4
 SLOT = 32
 STEP = 128
-EARLY = 1
+EARLY = 0
 BAND = 384
 VMEM_BYTES = 32 * 1024 * 1024
 F32 = jnp.float32
@@ -405,9 +405,9 @@
 
 def sparse_kernel(groups, radices, local, subs, cap, surplus, levels, comb_out, coef_out, lev_out, fits_out, *scratch):
     stages = len(radices)
-    (xh, xm, xs, ym, pm, csend, crecv, posm, lev, prod, cbuf, local_sem, m_sem, lev_sem, x_send,
-     x_recv) = scratch[:16]
-    rest = [scratch[16 + m * stages:16 + (m + 1) * stages] for m in range(6)]
+    (xh, xm, xs, ym, pm, csend, crecv, posm, lev, prod, local_sem, m_sem, lev_sem, x_send,
+     x_recv) = scratch[:15]
+    rest = [scratch[15 + m * stages:15 + (m + 1) * stages] for m in range(6)]
     slots, s_send, s_recv, own_slots, o_send, o_recv = rest
     grids = groups * local
     half = xh.shape[-1]
@@ -425,12 +425,7 @@
     loads = [pltpu.make_async_copy(surplus.at[:, :, cells[h]], xh.at[h], local_sem.at[h]) for h in range(2)]
     for load in loads:
         load.start()
-    turns = [
-        pltpu.make_async_copy(surplus.at[i, :, cells[h]], xm.at[h, :, i, :], m_sem.at[h, i])
-        for i in range(local) for h in range(2)
-    ]
-    for turn in turns:
-        turn.start()
+    turns = [pltpu.make_async_copy(surplus.at[i], xm.at[:, i, :], m_sem.at[i]) for i in range(local)]
 
     barrier = pltpu.get_barrier_semaphore()
     count = 0
@@ -473,47 +468,47 @@
                 xs[h, i:i + 256, m * half:(m + 1) * half] = part
 
     loads[0].wait()
+    for turn in turns:
+        turn.start()
     split_half(0)
+    def x_copy(h, ch):
+        rows = pl.ds(pl.multiple_of(ch * STEP, STEP), STEP)
+        return pltpu.make_async_remote_copy(
+            src_ref=csend.at[h, rows], dst_ref=crecv.at[h, rows], send_sem=x_send.at[h, ch], recv_sem=x_recv.at[h, ch],
+            device_id=(other, d), device_id_type=MESH,
+        )
+
+    index = lax.broadcasted_iota(jnp.int32, (256, 128), 0).astype(F32)
+
+    def gather_rows(h, first):
+        want = index + float(first)
+        acc = jnp.zeros((256, 3 * half), F32)
+        for m in range(0, len(pos_rows), 2):
+            picks = [jnp.where(want == p, 1.0, 0.0).astype(bf16) for p in pos_rows[m:m + 2]]
+            acc += jnp.dot(
+                jnp.concatenate(picks, axis=1), xs[h, m * 128:m * 128 + 256, :], preferred_element_type=F32
+            )
+        csend[h, first:first + 256, :] = acc[:, :half] + acc[:, half:2 * half] + acc[:, 2 * half:]
+
+    def depart(h, first, last):
+        for ch in range(first // STEP, last // STEP):
+            x_copy(h, ch).start()
+
+    gather_rows(0, 0)
     pl.semaphore_wait(barrier, count)
     lev_copy = pltpu.make_async_remote_copy(
         src_ref=lev.at[g], dst_ref=lev.at[g], send_sem=lev_sem.at[0], recv_sem=lev_sem.at[1],
         device_id=(other, d), device_id_type=MESH,
     )
     lev_copy.start()
-
-    def x_copy(h, ch):
-        rows = pl.ds(pl.multiple_of(ch * STEP, STEP), STEP)
-        return pltpu.make_async_remote_copy(
-            src_ref=csend.at[h, rows], dst_ref=crecv.at[h, rows], send_sem=x_send.at[h, ch], recv_sem=x_recv.at[h, ch],
-            device_id=(other, d), device_id_type=MESH,
-        )
-
-    index = lax.broadcasted_iota(jnp.int32, (STEP, 128), 0).astype(F32)
-
-    def gather_chunk(h, ch):
-        want = index + (ch * STEP).astype(F32)
-        acc = jnp.zeros((STEP, 3 * half), F32)
-        for m in range(0, len(pos_rows), 2):
-            picks = [jnp.where(want == p, 1.0, 0.0).astype(bf16) for p in pos_rows[m:m + 2]]
-            acc += jnp.dot(
-                jnp.concatenate(picks, axis=1), xs[h, m * 128:m * 128 + 256, :], preferred_element_type=F32
-            )
-        rows = pl.ds(pl.multiple_of(ch * STEP, STEP), STEP)
-        csend[h, rows, :] = acc[:, :half] + acc[:, half:2 * half] + acc[:, 2 * half:]
-
-    def send_chunk(h, ch, carry):
-        gather_chunk(h, ch)
-        x_copy(h, ch).start()
-        return carry
-
-    def hold_chunk(h, ch, carry):
-        gather_chunk(h, ch)
-        return carry
-
-    lax.fori_loop(0, chunks, functools.partial(send_chunk, 0), 0)
+    depart(0, 0, 256)
+    for first in range(256, cap, 256):
+        gather_rows(0, first)
+        depart(0, first, first + 256)
     loads[1].wait()
     split_half(1)
-    lax.fori_loop(0, EARLY, functools.partial(send_chunk, 1), 0)
+    gather_rows(1, 0)
+    depart(1, 0, EARLY)
 
     for turn in turns:
         turn.wait()
@@ -528,19 +523,16 @@
                 & (lev_out[1] >= lax.rem(s // 4, 4).astype(F32))
                 & (lev_out[2] >= float(k % 4))
             )
-            own = jnp.concatenate([own] * (half // 128), axis=1) if half > 128 else own
-            pair = [jnp.where(own, xm[h, s], 0.0) for h in range(2)]
-            for h in range(2):
-                xm[h, s] = pair[h]
-            y = split3_rows(jnp.concatenate(pair, axis=1))
-            ym[s] = y[:, half:]
+            own = jnp.concatenate([own] * (groups * half // 128), axis=1)
+            x = jnp.where(own, xm[s], 0.0)
+            xm[s] = x
+            y = split3_rows(x)
+            ym[s] = jnp.where(g == 0, y[:, :half], y[:, half:])
             total += outer(y, y)
         prod[...] += total
         return carry
 
     lax.fori_loop(0, subs // ROWS, own_gram, 0)
-    copies = spread_out(members, 0, own_slots[0], o_send[0], o_recv[0], pack(folded(prod[...], local)))
-    lax.fori_loop(EARLY, chunks, functools.partial(hold_chunk, 1), 0)
 
     lev_copy.wait_recv()
     keep = kept_by(lev_wide(other))
@@ -549,6 +541,8 @@
     for s in range(subs):
         posm[s * local:(s + 1) * local, :] = jnp.broadcast_to(pos[:, s:s + 1], (local, 128))
 
+    copies = spread_out(members, 0, own_slots[0], o_send[0], o_recv[0], pack(folded(prod[...], local)))
+
     def parts_at(h, first):
         return jnp.concatenate(parts_of(crecv[h, first:first + 256, :]), axis=1)
 
@@ -569,7 +563,7 @@
 
         for at in range(0, rows_all, BAND):
             y = placed(posm[at:at + BAND, :], first, parts, BAND)
-            pm[1, at:at + BAND, :] = y if first == 0 else pm[1, at:at + BAND, :] + y
+            pm[g, at:at + BAND, :] = y if first == 0 else pm[g, at:at + BAND, :] + y
 
     arrive(0, last)
     parts = parts_at(0, last)
@@ -577,8 +571,8 @@
     for at in range(0, rows_all, BAND):
         y = placed(posm[at:at + BAND, :], last, parts, BAND)
         if last > 0:
-            y = y + pm[1, at:at + BAND, :]
-        pm[1, at:at + BAND, :] = y
+            y = y + pm[g, at:at + BAND, :]
+        pm[g, at:at + BAND, :] = y
         for k in range(0, BAND // local, 2):
             s = at // local + k
             theirs = split3_rows(
@@ -593,14 +587,16 @@
             parts = parts_at(1, first)
             for at in range(0, rows_all, BAND):
                 y = placed(posm[at:at + BAND, :], first, parts, BAND)
-                pm[0, at:at + BAND, :] = y if first == 0 else pm[0, at:at + BAND, :] + y
+                pm[other, at:at + BAND, :] = y if first == 0 else pm[other, at:at + BAND, :] + y
 
     value = pack(folded(total, local))
     for t in range(stages):
         copies += spread_out(members, t, slots[t], s_send[t], s_recv[t], value)
         if t == 0:
-            for ch in range(EARLY, chunks):
-                x_copy(1, ch).start()
+            depart(1, EARLY, 256)
+            for first in range(256, cap, 256):
+                gather_rows(1, first)
+                depart(1, first, first + 256)
         gather_in(members, t, own_slots[t], o_send[t], o_recv[t])
         n = members[t][0]
         if t == 0:
@@ -633,15 +629,13 @@
     theirs = jnp.where(g == 0, coef_wide[local:], coef_wide[:local])
     if half > 128:
         ours, theirs = [jnp.concatenate([w] * (half // 128), axis=1) for w in (ours, theirs)]
-    for h, slot in ((0, other), (1, g)):
+    for h in range(groups):
         for first in range(0, subs, 8):
             at = first * local
-            acc = xm[h, first:first + 8] * ours[None] + (
+            acc = xm[first:first + 8, :, h * half:(h + 1) * half] * ours[None] + (
                 pm[h, at:at + 8 * local, :].reshape(8, local, half) * theirs[None]
             )
-            cbuf[slot, first:first + 8] = jnp.sum(acc, axis=1)
-    for h in range(groups):
-        comb_out[:, h * half:(h + 1) * half] = cbuf[h]
+            comb_out[first:first + 8, h * half:(h + 1) * half] = jnp.sum(acc, axis=1)
 
     for copy in copies:
         copy.wait_send()
@@ -725,7 +719,7 @@
         + (pl.BlockSpec(memory_space=pltpu.SMEM),),
         scratch_shapes=[
             pltpu.VMEM((2, local, subs, half), F32),
-            pltpu.VMEM((2, subs, local, half), F32),
+            pltpu.VMEM((subs, local, cells), F32),
             pltpu.VMEM((2, local * subs, 3 * half), jnp.bfloat16),
             pltpu.VMEM((subs, 3 * local, half), jnp.bfloat16),
             pltpu.VMEM((2, local * subs, half), F32),
@@ -734,8 +728,7 @@
             pltpu.VMEM((local * subs, 128), F32),
             pltpu.VMEM((groups, 3, local), jnp.int32),
             pltpu.VMEM((3 * local, 3 * local), F32),
-            pltpu.VMEM((groups, subs, half), F32),
-            dma((3,)), dma((2, local)), dma((2,)), dma((2, chunks)), dma((2, chunks)),
+            dma((3,)), dma((local,)), dma((2,)), dma((2, chunks)), dma((2, chunks)),
         ]
         + [pltpu.VMEM((n, 8, 128), F32) for n in sizes]
         + [dma((n,)) for n in sizes]

time: 28.9 us -> 27.9 us (0.965)
  Pallas kernels: 27.4 us -> 26.4 us
    pallas_call x1, Pallas kernels: 25.6 us -> 24.7 us  [sparse_call(): pl.pallas_call(functools.partial(sparse_kernel, groups, radices, local, s...]
where the time goes in v3:
time: 27.9 us; the launch traced here: 27.8 us
  Pallas kernels  26.4 us (95%)
  between operations  1.37 us (5%)
    pallas_call x1, Pallas kernels, sparse_call(): pl.pallas_call(functools.partial(sparse_kernel, groups, radices, local, s...  24.7 us
    pallas_call x1, Pallas kernels, shards(): pl.pallas_call(spread, out_shape=(jax.ShapeDtypeStruct((local, subs, cell...  1.74 us

profile of v3, /device:TPU:0, one launch (start us, length us, event | category | flops | bytes accessed | tf_op | source)
XLA Modules:
  0.0 27.8 jit_solution(6036208407397039803)
XLA Ops:
  0.6 0.0 copy-start
  0.6 0.0 copy-start.1
  0.6 24.7 %shard_map.41 = (f32[64,256]{1,0:T(8,128)S(1)}, f32[1,48]{1,0:T(1,128)S(1)}, f32[3,24,128]{2,1,0:T(8,128)S(1)}, s32[1,1]{1,0:T(1,128)}) custom-call(f32[24,64,256]{2,1,0:T(8,128)} %surplus.1, s32[3,24]{1,0:T(4,128)} %bitcast.3), custom_call_target="tpu_custom_call" | custom-call | tf_op jit(solution)/shard_map/pallas_call | solution.py:709
  26.0 0.0 copy-done
  26.0 0.0 copy-done.1
  26.0 1.7 %shard_map.42 = (f32[24,64,256]{2,1,0:T(8,128)}, f32[1,48]{1,0:T(1,128)}) custom-call(f32[64,256]{1,0:T(8,128)S(1)} %get-tuple-element.27.combined, f32[1,48]{1,0:T(1,128)S(1)} %get-tuple-element.28.coef, f32[3,24,128]{2,1,0:T(8,128)S(1)} %get-tuple-element.29.lev), custom_call_target="tpu_custom_call" | custom-call | tf_op jit(solution)/shard_map/pallas_call | solution.py:757
  (1 shorter events, 0.0 us)
Async XLA Ops:
  0.6 25.4 %copy-start = (f32[24,64,256]{2,1,0:T(8,128)S(1)}, f32[24,64,256]{2,1,0:T(8,128)}, u32[]{:S(2)}) copy-start(f32[24,64,256]{2,1,0:T(8,128)} %surplus.1) | copy-start | bytes 4718596
  0.6 25.4 %copy-start.1 = (s32[24,3]{0,1:T(4,128)S(1)}, s32[24,3]{0,1:T(4,128)}, u32[]{:S(2)}) copy-start(s32[24,3]{0,1:T(4,128)} %param.5) | copy-start | bytes 868

commit v4 on v3

--- a/solution.py
+++ b/solution.py
@@ -406,8 +406,8 @@
 def sparse_kernel(groups, radices, local, subs, cap, surplus, levels, comb_out, coef_out, lev_out, fits_out, *scratch):
     stages = len(radices)
     (xh, xm, xs, ym, pm, csend, crecv, posm, lev, prod, local_sem, m_sem, lev_sem, x_send,
-     x_recv) = scratch[:15]
-    rest = [scratch[15 + m * stages:15 + (m + 1) * stages] for m in range(6)]
+     x_recv, fits) = scratch[:16]
+    rest = [scratch[16 + m * stages:16 + (m + 1) * stages] for m in range(6)]
     slots, s_send, s_recv, own_slots, o_send, o_recv = rest
     grids = groups * local
     half = xh.shape[-1]
@@ -536,7 +536,9 @@
 
     lev_copy.wait_recv()
     keep = kept_by(lev_wide(other))
-    fits_out[0, 0] = jnp.where(jnp.maximum(own_count, jnp.sum(keep)) <= float(cap), 1, 0)
+    fits[0, 0] = jnp.where(jnp.maximum(own_count, jnp.sum(keep)) <= float(cap), 1, 0)
+    fits_copy = pltpu.make_async_copy(fits, fits_out, local_sem.at[3])
+    fits_copy.start()
     pos = places_of(keep, True)
     for s in range(subs):
         posm[s * local:(s + 1) * local, :] = jnp.broadcast_to(pos[:, s:s + 1], (local, 128))
@@ -637,6 +639,7 @@
             )
             comb_out[first:first + 8, h * half:(h + 1) * half] = jnp.sum(acc, axis=1)
 
+    fits_copy.wait()
     for copy in copies:
         copy.wait_send()
     lev_copy.wait_send()
@@ -716,7 +719,7 @@
         ),
         in_specs=[pl.BlockSpec(memory_space=pltpu.HBM), pl.BlockSpec(memory_space=pltpu.HBM)],
         out_specs=tuple(pl.BlockSpec(memory_space=pltpu.VMEM) for _ in range(3))
-        + (pl.BlockSpec(memory_space=pltpu.SMEM),),
+        + (pl.BlockSpec(memory_space=pltpu.HBM),),
         scratch_shapes=[
             pltpu.VMEM((2, local, subs, half), F32),
             pltpu.VMEM((subs, local, cells), F32),
@@ -728,7 +731,8 @@
             pltpu.VMEM((local * subs, 128), F32),
             pltpu.VMEM((groups, 3, local), jnp.int32),
             pltpu.VMEM((3 * local, 3 * local), F32),
-            dma((3,)), dma((local,)), dma((2,)), dma((2, chunks)), dma((2, chunks)),
+            dma((4,)), dma((local,)), dma((2,)), dma((2, chunks)), dma((2, chunks)),
+            pltpu.SMEM((1, 1), jnp.int32),
         ]
         + [pltpu.VMEM((n, 8, 128), F32) for n in sizes]
         + [dma((n,)) for n in sizes]

time: 27.9 us -> 27.4 us (0.982)
  Pallas kernels: 26.4 us -> 25.9 us
    pallas_call x1, Pallas kernels: 24.7 us -> 24.2 us  [sparse_call(): pl.pallas_call(functools.partial(sparse_kernel, groups, radices, local, s...]
where the time goes in v4:
time: 27.4 us; the launch traced here: 27.3 us
  Pallas kernels  25.9 us (95%)
  between operations  1.37 us (5%)
    pallas_call x1, Pallas kernels, sparse_call(): pl.pallas_call(functools.partial(sparse_kernel, groups, radices, local, s...  24.2 us
    pallas_call x1, Pallas kernels, shards(): pl.pallas_call(spread, out_shape=(jax.ShapeDtypeStruct((local, subs, cell...  1.74 us

profile of v4, /device:TPU:0, one launch (start us, length us, event | category | flops | bytes accessed | tf_op | source)
XLA Modules:
  0.0 27.3 jit_solution(6102539127916292578)
XLA Ops:
  0.6 0.0 copy-start
  0.6 0.0 copy-start.1
  0.6 24.2 %shard_map.41 = (f32[64,256]{1,0:T(8,128)S(1)}, f32[1,48]{1,0:T(1,128)S(1)}, f32[3,24,128]{2,1,0:T(8,128)S(1)}, s32[1,1]{1,0:T(1,128)}) custom-call(f32[24,64,256]{2,1,0:T(8,128)} %surplus.1, s32[3,24]{1,0:T(4,128)} %bitcast.3), custom_call_target="tpu_custom_call" | custom-call | tf_op jit(solution)/shard_map/pallas_call | solution.py:712
  25.5 0.0 copy-done
  25.5 0.0 copy-done.1
  25.5 1.7 %shard_map.42 = (f32[24,64,256]{2,1,0:T(8,128)}, f32[1,48]{1,0:T(1,128)}) custom-call(f32[64,256]{1,0:T(8,128)S(1)} %get-tuple-element.27.combined, f32[1,48]{1,0:T(1,128)S(1)} %get-tuple-element.28.coef, f32[3,24,128]{2,1,0:T(8,128)S(1)} %get-tuple-element.29.lev), custom_call_target="tpu_custom_call" | custom-call | tf_op jit(solution)/shard_map/pallas_call | solution.py:761
  (1 shorter events, 0.0 us)
Async XLA Ops:
  0.6 24.9 %copy-start = (f32[24,64,256]{2,1,0:T(8,128)S(1)}, f32[24,64,256]{2,1,0:T(8,128)}, u32[]{:S(2)}) copy-start(f32[24,64,256]{2,1,0:T(8,128)} %surplus.1) | copy-start | bytes 4718596
  0.6 24.9 %copy-start.1 = (s32[24,3]{0,1:T(4,128)S(1)}, s32[24,3]{0,1:T(4,128)}, u32[]{:S(2)}) copy-start(s32[24,3]{0,1:T(4,128)} %param.5) | copy-start | bytes 868
